TPU v7x, 32 devices: a whole 2x2x4 slice. The times are simulated.
32 devices in a mesh: row: 8 (over z, core), rep: 4 (over y, x).
Axes of the slice: x: 2, y: 2, z: 4, core: 2. Of those that a mesh axis runs over, the one named last changes fastest.
Arguments:
- basis: bfloat16 [32, 65536], P(None, ('row', 'rep')), may hold values from -6 to 6
- precond: float32 [65536], P(('row', 'rep')), may hold values from 0.1 to 0.4
- tiles: bfloat16 [1024, 256, 256], P(('row', 'rep')), as said below
- tile_rows: int32 [1024], P(('row', 'rep')), may hold values from 0 to 31, as said below
- tile_cols: int32 [1024], P(('row', 'rep')), may hold values from 0 to 63, as said below
Outputs:
- directions: float32 [32, 65536], P(None, ('row', 'rep'))
- projected: float32 [64, 64], replicated
Inputs may be any that keep to these rules, and one draw needn't show every extreme that they name: The matrix A assembled from all tiles as the steps say is symmetric. `tile_rows`: each device's 32 entries index tile-rows of its band, which are held by the devices of its index along row, in the order of rep. The first 8 entries of a device are its diagonal tiles: the t-th is (index along rep) * 8 + t. Of the other entries none falls in the device's own index along rep, and at most 8 fall in the tile-rows of any one other index along rep, exactly 8 for some. `tile_cols`: each device's 32 entries index tile-columns held by the devices of its index along rep, in the order of row. The first 8 entries of a device are (index along row) * 8 + t for the t-th. Of the other entries none falls in the device's own index along row, and at most 4 fall in the tile-columns of any one other index along row, exactly 4 for some.
All inputs are finite; a program needn't handle non-finite values.
Results may differ from a plain program's by a relative error of at most 0.0003.
Values sent between devices are 32-bit elements; how exact they have to be, the bound alone decides.
No kernel may reach another device: no remote copies, remote signals or barrier semaphores. Data moves between devices by JAX's collectives and lax.ppermute only.
A program may use at most 64 MiB of HBM per device.

v0:
```python
import jax
import jax.numpy as jnp
from jax import lax
from jax.sharding import PartitionSpec as P


def shards(basis, precond, tiles, tile_rows, tile_cols):
    highest = lax.Precision.HIGHEST
    columns = basis.shape[0]
    shard_rows = basis.shape[1]
    tile_size = tiles.shape[1]
    tiles_each = shard_rows // tile_size
    row_count = lax.axis_size("row")
    rep_count = lax.axis_size("rep")
    inverse_count = 1.0 / (shard_rows * row_count * rep_count)
    basis_float = basis.astype(jnp.float32)

    def apply_matrix(vectors):
        gathered = lax.all_gather(vectors, "row", axis=1, tiled=True)
        blocks = gathered.reshape(columns, -1, tile_size)
        picked = jnp.take(blocks, tile_cols, axis=1)
        products = jnp.einsum(
            "kjc,jrc->kjr", picked, tiles, precision=highest, preferred_element_type=jnp.float32
        )
        selector = (
            tile_rows[:, None] == jnp.arange(rep_count * tiles_each, dtype=jnp.int32)[None, :]
        ).astype(jnp.float32)
        partial_value = jnp.einsum("kjr,jb->kbr", products, selector, precision=highest).reshape(
            columns, -1
        )
        summed = lax.psum_scatter(partial_value, "rep", scatter_dimension=1, tiled=True)
        return summed

    applied = apply_matrix(basis_float)
    basis_applied, basis_gram, scaled_applied, scaled_gram = lax.psum(
        (
            jnp.dot(applied, basis_float.T, precision=highest),
            jnp.dot(basis_float, basis_float.T, precision=highest),
            jnp.dot(precond[None, :] * applied, basis_float.T, precision=highest),
            jnp.dot(precond[None, :] * basis_float, basis_float.T, precision=highest),
        ),
        ("row", "rep"),
    )
    basis_applied = basis_applied * inverse_count
    basis_gram = basis_gram * inverse_count
    scaled_applied = scaled_applied * inverse_count
    scaled_gram = scaled_gram * inverse_count
    ritz_values = jnp.diagonal(basis_applied)
    residual = applied - ritz_values[:, None] * basis_float
    correlation = basis_applied - ritz_values[:, None] * basis_gram
    right_side = -(residual - jnp.dot(correlation, basis_float, precision=highest))
    seeded = precond[None, :] * right_side
    coefficients = (
        -scaled_applied
        + ritz_values[:, None] * scaled_gram
        + jnp.dot(correlation, scaled_gram, precision=highest)
    )
    correction = seeded - jnp.dot(coefficients, basis_float, precision=highest)
    image_block = apply_matrix(correction)
    updated = correction + precond[None, :] * (
        right_side - (image_block - ritz_values[:, None] * correction)
    )
    coefficients = (
        lax.psum(jnp.dot(updated, basis_float.T, precision=highest), ("row", "rep")) * inverse_count
    )
    correction = updated - jnp.dot(coefficients, basis_float, precision=highest)
    correction_gram = (
        lax.psum(jnp.dot(correction, correction.T, precision=highest), ("row", "rep"))
        * inverse_count
    )
    factor = jnp.linalg.cholesky(correction_gram)
    directions = lax.linalg.triangular_solve(factor, correction, left_side=True, lower=True)
    adirections = apply_matrix(directions)
    block_cross, block_new = lax.psum(
        (
            jnp.dot(basis_float, adirections.T, precision=highest),
            jnp.dot(directions, adirections.T, precision=highest),
        ),
        ("row", "rep"),
    )
    block_basis = basis_applied.T
    block_cross = block_cross * inverse_count
    block_new = block_new * inverse_count
    upper = jnp.concatenate([block_basis, block_cross], axis=1)
    lower = jnp.concatenate([block_cross.T, block_new], axis=1)
    projected = jnp.concatenate([upper, lower], axis=0)
    return (directions, projected)


def solution(mesh):
    in_specs = (
        P(None, ("row", "rep")),
        P(("row", "rep")),
        P(("row", "rep"), None, None),
        P(("row", "rep")),
        P(("row", "rep")),
    )
    out_specs = (P(None, ("row", "rep")), P())
    return jax.shard_map(shards, mesh=mesh, in_specs=in_specs, out_specs=out_specs, check_vma=False)
```

profile of v0, /device:TPU:0, one launch (start us, length us, event | category | flops | bytes accessed | tf_op | source)
XLA Modules:
  0.0 404.3 jit_solution(3275657907791590725)
XLA Ops:
  7.2 1.6 convert_element_type.2
  10.2 31.8 %all-gather.4.cloned.1.call-done = f32[32,16384]{1,0:T(8,128)} async-done(((f32[32,2048]{1,0:T(8,128)}), f32[32,16384]{1,0:T(8,128)}) %all-gather.4.cloned.1.call-update) | async-done | bytes 2097168 | tf_op jit(solution)/shard_map/all_gather | solution.py:19
  42.1 1.9 copy.54
  44.6 5.9 %fusion.11 = f32[32,32,256]{2,1,0:T(8,128)S(1)} fusion(bf16[32,256,256]{2,1,0:T(8,128)(2,1)} %param.9, f32[32,32,256]{2,1,0:T(8,128)S(1)} %gather_fusion.1, pred[32]{0:T(512)(128)(4,1)S(1)} %compare_and_fusion), kind=kOutput, calls=%fused_computation.23 | convolution fusion | flops 805568512 | bytes 6291488 | tf_op jit(solution)/shard_map/kjc,jrc->kjr/dot_general | solution.py:22
  50.6 1.3 fusion.9
  51.8 1.6 copy.34
  54.0 27.0 %reduce-scatter.4.cloned.1.call-done = f32[32,2048]{1,0:T(8,128)} async-done(((f32[32,8192]{1,0:T(8,128)}), f32[32,2048]{1,0:T(8,128)}) %reduce-scatter.4.cloned.1.call-update) | async-done | bytes 262160 | tf_op jit(solution)/shard_map/reduce_scatter | solution.py:31
  81.0 1.2 fusion.27
  82.2 1.2 fusion.54
  83.4 40.0 %all-reduce.1 = (f32[32,32]{1,0:T(8,128)S(1)}, f32[32,32]{1,0:T(8,128)S(1)}, f32[32,32]{1,0:T(8,128)S(1)}, f32[32,32]{1,0:T(8,128)S(1)}) all-reduce(f32[32,32]{1,0:T(8,128)S(1)} %fusion.25, f32[32,32]{1,0:T(8,128)S(1)} %fusion.27, f32[32,32]{1,0:T(8,128)S(1)} %fusion.54, ...), channel_id=1, replica_groups=mesh['row'=8,'rep'=4] {'row','rep'}, use_global_device_ids=true, to_apply=%region_4.6 | all-reduce | flops 4096 | bytes 32768 | tf_op jit(solution)/shard_map/psum | solution.py:35
  124.9 1.3 fusion
  127.3 30.0 %all-gather.6.cloned.1.call-done = f32[32,16384]{1,0:T(8,128)} async-done(((f32[32,2048]{1,0:T(8,128)}), f32[32,16384]{1,0:T(8,128)}) %all-gather.6.cloned.1.call-update) | async-done | bytes 2097168 | tf_op jit(solution)/shard_map/all_gather | solution.py:19
  157.3 1.9 copy.53
  159.8 5.9 %fusion.7 = f32[32,32,256]{2,1,0:T(8,128)S(1)} fusion(bf16[32,256,256]{2,1,0:T(8,128)(2,1)} %param.9, f32[32,32,256]{2,1,0:T(8,128)S(1)} %gather_fusion.2, pred[32]{0:T(512)(128)(4,1)} %copy-done.6), kind=kOutput, calls=%fused_computation.19 | convolution fusion | flops 805568512 | bytes 6291488 | tf_op jit(solution)/shard_map/kjc,jrc->kjr/dot_general | solution.py:22
  165.8 1.3 fusion.5
  167.0 1.6 copy.35
  168.9 27.3 %reduce-scatter.6.cloned.1.call-done = f32[32,2048]{1,0:T(8,128)} async-done(((f32[32,8192]{1,0:T(8,128)}), f32[32,2048]{1,0:T(8,128)}) %reduce-scatter.6.cloned.1.call-update) | async-done | bytes 262160 | tf_op jit(solution)/shard_map/reduce_scatter | solution.py:31
  196.1 1.1 multiply_add_fusion
  197.5 39.3 %psum.60 = f32[32,32]{0,1:T(8,128)S(1)} all-reduce(f32[32,32]{0,1:T(8,128)S(1)} %fusion.56), channel_id=1, replica_groups=mesh['row'=8,'rep'=4] {'row','rep'}, use_global_device_ids=true, to_apply=%region_6.8 | all-reduce | flops 1024 | bytes 8192 | tf_op jit(solution)/shard_map/psum | solution.py:64
  237.5 41.1 %psum.61 = f32[32,32]{0,1:T(8,128)S(1)} all-reduce(f32[32,32]{0,1:T(8,128)S(1)} %fusion.57), channel_id=1, replica_groups=mesh['row'=8,'rep'=4] {'row','rep'}, use_global_device_ids=true, to_apply=%region_7.9 | all-reduce | flops 1024 | bytes 8192 | tf_op jit(solution)/shard_map/psum | solution.py:68
  278.7 2.9 cholesky.16
  283.0 2.4 custom-call.6
  285.4 1.1 fusion.33
  286.6 29.0 %all-gather.8.cloned.1.call-done = f32[32,16384]{1,0:T(8,128)} async-done(((f32[32,2048]{1,0:T(8,128)}), f32[32,16384]{1,0:T(8,128)}) %all-gather.8.cloned.1.call-update) | async-done | bytes 2097168 | tf_op jit(solution)/shard_map/all_gather | solution.py:19
  315.7 1.9 copy.52
  318.2 5.9 %fusion.3 = f32[32,32,256]{2,1,0:T(8,128)S(1)} fusion(bf16[32,256,256]{2,1,0:T(8,128)(2,1)} %param.9, f32[32,32,256]{2,1,0:T(8,128)S(1)} %gather_fusion.3, pred[32]{0:T(512)(128)(4,1)S(1)} %copy-done.7), kind=kOutput, calls=%fused_computation.15 | convolution fusion | flops 805568512 | bytes 6291488 | tf_op jit(solution)/shard_map/kjc,jrc->kjr/dot_general | solution.py:22
  324.2 1.3 fusion.1
  325.4 1.6 copy.36
  327.1 27.5 %reduce-scatter.8.cloned.1.call-done = f32[32,2048]{1,0:T(8,128)} async-done(((f32[32,8192]{1,0:T(8,128)}), f32[32,2048]{1,0:T(8,128)}) %reduce-scatter.8.cloned.1.call-update) | async-done | bytes 262160 | tf_op jit(solution)/shard_map/reduce_scatter | solution.py:31
  354.6 1.3 fusion.58
  355.9 1.2 convolution_bitcast_fusion
  357.1 39.5 %all-reduce = (f32[32,32]{0,1:T(8,128)S(1)}, f32[32,32]{0,1:T(8,128)S(1)}) all-reduce(f32[32,32]{0,1:T(8,128)S(1)} %fusion.58, f32[32,32]{0,1:T(8,128)S(1)} %convolution_bitcast_fusion), channel_id=1, replica_groups=mesh['row'=8,'rep'=4] {'row','rep'}, use_global_device_ids=true, to_apply=%region_12.14 | all-reduce | flops 2048 | bytes 16384 | tf_op jit(solution)/shard_map/psum | solution.py:74
  (59 shorter events, 9.9 us)
Async XLA Ops:
  7.2 34.9 %all-gather.4.cloned.1.call-start = ((), (), s32[]{:S(2)}) async-start(), calls=%async_computation.3 | async-start | bytes 2359296 | tf_op jit(solution)/shard_map/all_gather | solution.py:19
  8.9 72.1 %reduce-scatter.4.cloned.1.call-start = ((), (), s32[]{:S(2)}) async-start(), calls=%async_computation.4 | async-start | bytes 1310720 | tf_op jit(solution)/shard_map/reduce_scatter | solution.py:31
  10.2 34.3 %copy-start.6 = (pred[32]{0:T(512)(128)(4,1)}, pred[32]{0:T(512)(128)(4,1)S(1)}, u32[]{:S(2)}) copy-start(pred[32]{0:T(512)(128)(4,1)S(1)} %compare_and_fusion) | copy-start | bytes 100
  43.9 6.6 %copy-start.5 = (s32[32]{0:T(128)S(1)}, s32[32]{0:T(128)}, u32[]{:S(2)}) copy-start(s32[32]{0:T(128)} %param.10) | copy-start | bytes 388
  50.5 3.0 copy-start
  50.6 3.1 copy-start.3
  53.5 103.8 %all-gather.6.cloned.1.call-start = ((), (), s32[]{:S(2)}) async-start(), calls=%async_computation.5 | async-start | bytes 2359296 | tf_op jit(solution)/shard_map/all_gather | solution.py:19
  124.7 32.5 %copy-start.8 = (f32[32]{0:T(128)}, f32[32]{0:T(128)S(1)}, u32[]{:S(2)}) copy-start(f32[32]{0:T(128)S(1)} %gather_fusion) | copy-start | bytes 388
  127.2 68.9 %reduce-scatter.6.cloned.1.call-start = ((), (), s32[]{:S(2)}) async-start(), calls=%async_computation.6 | async-start | bytes 1310720 | tf_op jit(solution)/shard_map/reduce_scatter | solution.py:31
  165.7 30.4 %copy-start.2 = (f32[32,2048]{1,0:T(8,128)S(1)}, f32[32,2048]{1,0:T(8,128)}, u32[]{:S(2)}) copy-start(f32[32,2048]{1,0:T(8,128)} %convolution_subtract_fusion.1) | copy-start | bytes 786436
  165.7 30.4 %copy-start.9 = (f32[32]{0:T(128)S(1)}, f32[32]{0:T(128)}, u32[]{:S(2)}) copy-start(f32[32]{0:T(128)} %copy-done.8) | copy-start | bytes 388
  168.6 147.0 %all-gather.8.cloned.1.call-start = ((), (), s32[]{:S(2)}) async-start(), calls=%async_computation.7 | async-start | bytes 2359296 | tf_op jit(solution)/shard_map/all_gather | solution.py:19
  236.8 81.4 %copy-start.7 = (pred[32]{0:T(512)(128)(4,1)S(1)}, pred[32]{0:T(512)(128)(4,1)}, u32[]{:S(2)}) copy-start(pred[32]{0:T(512)(128)(4,1)} %copy-done.6) | copy-start | bytes 100
  286.6 68.0 %reduce-scatter.8.cloned.1.call-start = ((), (), s32[]{:S(2)}) async-start(), calls=%async_computation.8 | async-start | bytes 1310720 | tf_op jit(solution)/shard_map/reduce_scatter | solution.py:31
  324.1 30.4 %copy-start.1 = (f32[32,2048]{1,0:T(8,128)S(1)}, f32[32,2048]{1,0:T(8,128)}, u32[]{:S(2)}) copy-start(f32[32,2048]{1,0:T(8,128)} %fusion.33) | copy-start | bytes 786436
  324.2 72.5 %copy-start.4 = (f32[32,32]{0,1:T(8,128)S(1)}, f32[32,32]{0,1:T(8,128)}, u32[]{:S(2)}) copy-start(f32[32,32]{0,1:T(8,128)} %get-tuple-element.13) | copy-start | bytes 12292
Sparse Core Ops, SparseCore 0:
  10.1 31.8 all-gather.3
  53.6 27.3 reduce-scatter.3
  127.3 29.8 all-gather.5
  168.8 27.3 reduce-scatter.5
  286.7 28.9 all-gather.7
  327.2 27.3 reduce-scatter.7
where the time goes:
time: 405 us; the launch traced here: 404 us
  waiting for transfers between devices  173 us (43%)
  blocking collectives  160 us (40%)
  matrix products  31.4 us (8%)
  between operations  14.4 us (4%)
  local copies, waits for them, and re-layouts  13.9 us (3%)
  other arithmetic  11.4 us (3%)
    all_gather x3, waiting for transfers between devices, apply_matrix(): gathered = lax.all_gather(vectors, 'row', axis=1, tiled=True)  90.9 us
    reduce_scatter x3, waiting for transfers between devices, apply_matrix(): lax.psum_scatter(partial_value, 'rep', scatter_dimension=1, tiled=True)  81.7 us
    psum x1, blocking collectives, shards(): lax.psum(jnp.dot(correction, correction.T, precision=highest), ('row', 'r...  41.1 us
    psum x1, blocking collectives, shards(): lax.psum((jnp.dot(applied, basis_float.T, precision=highest), jnp.dot(bas...  40 us
    psum x1, blocking collectives, shards(): lax.psum((jnp.dot(basis_float, adirections.T, precision=highest), jnp.dot...  39.5 us
    psum x1, blocking collectives, shards(): lax.psum(jnp.dot(updated, basis_float.T, precision=highest), ('row', 'rep'))  39.3 us
    dot_general x3, matrix products, apply_matrix(): jnp.einsum('kjc,jrc->kjr', picked, tiles, precision=highest, preferred_el...  17.8 us
  transfers between devices with their start and end apart: 6, of which 6 were waited for; matrix products, arithmetic and copies ran while one was open for 0% of the time, Pallas kernels for 0%

commit v1 on v0

v1 whole, which is shorter than its diff:
```python
import functools
import jax
import jax.numpy as jnp
from jax import lax
from jax.experimental import pallas as pl
from jax.experimental.pallas import tpu as pltpu
from jax.sharding import PartitionSpec as P

F32 = jnp.float32
BF16 = jnp.bfloat16
HIGHEST = lax.Precision.HIGHEST
ROW, REP = "row", "rep"


def xor_move(value, axis, mask):
    count = lax.axis_size(axis)
    return lax.ppermute(value, axis, [(i, i ^ mask) for i in range(count)])


def split(value, terms):
    parts = []
    rest = value
    for i in range(terms):
        part = rest.astype(BF16)
        parts.append(part)
        if i + 1 < terms:
            rest = rest - part.astype(F32)
    return parts


def fold(value, rows):
    total = value[:rows]
    for i in range(1, value.shape[0] // rows):
        total = total + value[i * rows : (i + 1) * rows]
    return total


def dot_nt(left, right):
    return lax.dot_general(left, right, (((1,), (1,)), ((), ())), preferred_element_type=F32)


def dot_nn(left, right):
    return lax.dot_general(left, right, (((1,), (0,)), ((), ())), preferred_element_type=F32)


def small_nt(left, right):
    rows = left.shape[0]
    stacked = jnp.concatenate(split(left, 3), axis=0)
    total = None
    for part in split(right, 3):
        one = dot_nt(stacked, part)
        total = one if total is None else total + one
    return fold(total, rows)


def full_dot(left, right):
    return jnp.dot(left, right, precision=HIGHEST, preferred_element_type=F32)


def full_nt(left, right):
    return lax.dot_general(
        left, right, (((1,), (1,)), ((), ())), precision=HIGHEST, preferred_element_type=F32
    )


VMEM = pl.BlockSpec(memory_space=pltpu.VMEM)
SMEM = pl.BlockSpec(memory_space=pltpu.SMEM)


def call(kernel, name, outs, smem, args, scratch=()):
    return pl.pallas_call(
        kernel,
        name=name,
        out_shape=[jax.ShapeDtypeStruct(s, d) for s, d in outs],
        in_specs=[SMEM] * smem + [VMEM] * (len(args) - smem),
        out_specs=[VMEM] * len(outs),
        scratch_shapes=list(scratch),
    )(*args)


def multiply_tiles(index_of, rows_ref, tiles_ref, xs_ref, acc_ref, rep, tiles_each, columns, group=4):
    tile_count = tiles_ref.shape[0]

    def step(g, carry):
        products = []
        for i in range(group):
            j = g * group + i
            slot, weight = index_of(j)
            product = fold(dot_nt(xs_ref[slot], tiles_ref[j]), columns)
            if weight is not None:
                product = product * weight
            products.append(product)
        for i in range(group):
            row = rows_ref[g * group + i]
            place = lax.bitwise_xor(row // tiles_each, rep) * tiles_each + row % tiles_each
            acc_ref[place] = acc_ref[place] + products[i]
        return carry

    lax.fori_loop(0, tile_count // group, step, 0)


def fill_terms(x_refs, xs_ref, tiles_each, columns, terms):
    for m, x_ref in enumerate(x_refs):

        def one(t, carry, m=m, x_ref=x_ref):
            for i, part in enumerate(split(x_ref[t], terms)):
                xs_ref[m * tiles_each + t, i * columns : (i + 1) * columns, :] = part
            return carry

        lax.fori_loop(0, tiles_each, one, 0)


def shards(basis, precond, tiles, tile_rows, tile_cols):
    columns = basis.shape[0]
    shard_rows = basis.shape[1]
    tile_size = tiles.shape[1]
    tiles_each = shard_rows // tile_size
    row_count = lax.axis_size(ROW)
    rep_count = lax.axis_size(REP)
    chips = row_count // 2
    inverse_count = 1.0 / (shard_rows * row_count * rep_count)
    block = (tiles_each, columns, tile_size)
    small = (columns, columns)
    band_slots = rep_count * tiles_each
    place = jnp.stack([lax.axis_index(ROW), lax.axis_index(REP)]).astype(jnp.int32)
    scaling = precond.reshape(tiles_each, 1, tile_size)

    def groups(bits):
        return [bits[i : i + 2] for i in range(0, len(bits), 2)]

    def sum_over(value, axis, bits):
        if len(bits) == 1:
            return value + xor_move(value, axis, bits[0])
        one, two = bits
        near = xor_move(value, axis, one)
        far = xor_move(value, axis, two)
        both = xor_move(value, axis, one | two)
        return (value + near) + (far + both)

    def bits_of(count, first):
        return [1 << i for i in range(first, count.bit_length() - 1)]

    def sum_all(value):
        value = sum_over(value, ROW, [1])
        for bits in groups(bits_of(rep_count, 0)):
            value = sum_over(value, REP, bits)
        for bits in groups(bits_of(row_count, 1)):
            value = sum_over(value, ROW, bits)
        return value

    def gather_row(value):
        same = [value] + [xor_move(value, ROW, 2 * k) for k in range(1, chips)]
        other = [xor_move(v, ROW, 1) for v in same]
        return [v for pair in zip(same, other) for v in pair]

    def gather_rep(value):
        return [value] + [xor_move(value, REP, k) for k in range(1, rep_count)]

    def scatter_rep(parts):
        return [parts[0]] + [xor_move(parts[k], REP, k) for k in range(1, rep_count)]

    pad_rows = 8

    def prepare_kernel(basis_ref, scaling_ref, block_ref, band_ref):
        for t in range(tiles_each):
            value = basis_ref[:, t * tile_size : (t + 1) * tile_size].astype(F32)
            block_ref[t] = value
            band_ref[t, :columns, :] = value
            band_ref[t, columns:, :] = jnp.broadcast_to(scaling_ref[t], (pad_rows, tile_size))

    basis_block, basis_band = call(
        prepare_kernel,
        "prepare",
        [(block, F32), ((tiles_each, columns + pad_rows, tile_size), F32)],
        0,
        (basis, scaling),
    )

    def product_kernel(terms, with_band):
        def kernel(place_ref, rows_ref, cols_ref, tiles_ref, *refs):
            x_refs, refs = refs[:row_count], refs[row_count:]
            if with_band:
                band_refs, refs = refs[:rep_count], refs[rep_count:]
            out_refs, refs = refs[:rep_count], refs[rep_count:]
            if with_band:
                small_ref, refs = refs[0], refs[1:]
            xs_ref, acc_ref = refs
            row, rep = place_ref[0], place_ref[1]
            fill_terms(x_refs, xs_ref, tiles_each, columns, terms)
            acc_ref[...] = jnp.zeros(acc_ref.shape, F32)

            def index_of(j):
                col = cols_ref[j]
                slot = lax.bitwise_xor(col // tiles_each, row) * tiles_each + col % tiles_each
                return slot, None

            multiply_tiles(index_of, rows_ref, tiles_ref, xs_ref, acc_ref, rep, tiles_each, columns)
            for k in range(rep_count):
                out_refs[k][...] = acc_ref[k * tiles_each : (k + 1) * tiles_each]
            if with_band:
                totals = [jnp.zeros((3 * columns, columns), F32)] * 2
                for k in range(rep_count):

                    def one(t, carry, k=k):
                        plain, scaled = carry
                        left = jnp.concatenate(split(acc_ref[k * tiles_each + t], 3), axis=0)
                        rows = band_refs[k][t, :columns, :]
                        plain = plain + dot_nt(left, rows.astype(BF16))
                        weighted = rows * band_refs[k][t, columns : columns + 1, :]
                        for part in split(weighted, 3):
                            scaled = scaled + dot_nt(left, part)
                        return plain, scaled

                    totals = lax.fori_loop(0, tiles_each, one, tuple(totals))
                own = [jnp.zeros((columns, columns), F32), jnp.zeros((3 * columns, columns), F32)]
                for t in range(tiles_each):
                    rows = band_refs[0][t, :columns, :]
                    weighted = rows * band_refs[0][t, columns : columns + 1, :]
                    narrow = rows.astype(BF16)
                    own[0] = own[0] + dot_nt(narrow, narrow)
                    own[1] = own[1] + dot_nt(jnp.concatenate(split(weighted, 3), axis=0), narrow)
                pieces = [fold(totals[0], columns), fold(totals[1], columns), own[0], fold(own[1], columns)]
                small_ref[...] = jnp.concatenate([p * inverse_count for p in pieces], axis=1)

        return kernel

    def products(x_blocks, band, terms):
        with_band = band is not None
        outs = [(block, F32)] * rep_count
        if with_band:
            outs = outs + [((columns, 4 * columns), F32)]
        return call(
            product_kernel(terms, with_band),
            "products_band" if with_band else "products",
            outs,
            3,
            (place, tile_rows, tile_cols, tiles, *x_blocks, *(band or ())),
            [
                pltpu.VMEM((row_count * tiles_each, terms * columns, tile_size), BF16),
                pltpu.VMEM((band_slots, columns, tile_size), F32),
            ],
        )

    row_blocks = gather_row(basis_block)
    band_blocks = gather_rep(basis_band)
    *partial, small_local = products(row_blocks, band_blocks, 1)
    received = scatter_rep(partial)
    basis_small = sum_all(small_local)

    def correct_kernel(small_ref, basis_ref, scaling_ref, *refs):
        parts, (applied_ref, right_ref, correction_ref, ritz_ref) = refs[:rep_count], refs[rep_count:]
        applied_small = small_ref[:, :columns]
        scaled_small = small_ref[:, columns : 2 * columns]
        gram = small_ref[:, 2 * columns : 3 * columns]
        scaled_gram = small_ref[:, 3 * columns : 4 * columns]
        down = lax.broadcasted_iota(jnp.int32, small, 0)
        across = lax.broadcasted_iota(jnp.int32, small, 1)
        diagonal = jnp.where(down == across, applied_small, 0.0)
        ritz = jnp.sum(diagonal, axis=1, keepdims=True)
        correlation = applied_small - ritz * gram
        coefficients = -scaled_small + ritz * scaled_gram + full_dot(correlation, scaled_gram)
        mix = correlation + diagonal
        stacked = jnp.concatenate(split(mix, 3) + split(coefficients, 3), axis=0)
        for t in range(tiles_each):
            total = parts[0][t]
            for part in parts[1:]:
                total = total + part[t]
            applied_ref[t] = total
            mixed = dot_nn(stacked, basis_ref[t].astype(BF16))
            right = fold(mixed[: 3 * columns], columns) - total
            right_ref[t] = right
            correction_ref[t] = scaling_ref[t] * right - fold(mixed[3 * columns :], columns)
        ritz_ref[...] = ritz

    applied, right_side, correction, ritz = call(
        correct_kernel,
        "correct",
        [(block, F32), (block, F32), (block, F32), ((columns, 1), F32)],
        0,
        (basis_small, basis_block, scaling, *received),
    )

    received = scatter_rep(products(gather_row(correction), None, 3))

    def update_kernel(ritz_ref, basis_ref, scaling_ref, applied_ref, right_ref, correction_ref, *refs):
        parts, (updated_ref, small_ref) = refs[:rep_count], refs[rep_count:]
        ritz = ritz_ref[...]
        totals = [jnp.zeros((3 * columns, columns), F32)] * 3
        for t in range(tiles_each):
            image = parts[0][t]
            for part in parts[1:]:
                image = image + part[t]
            start = correction_ref[t]
            updated = start + scaling_ref[t] * (right_ref[t] - (image - ritz * start))
            updated_ref[t] = updated
            terms = split(updated, 3)
            left = jnp.concatenate(terms, axis=0)
            totals[0] = totals[0] + dot_nt(left, basis_ref[t].astype(BF16))
            for term in terms:
                totals[1] = totals[1] + dot_nt(left, term)
            for term in split(applied_ref[t], 3):
                totals[2] = totals[2] + dot_nt(left, term)
        pieces = [fold(total, columns) * inverse_count for total in totals]
        small_ref[...] = jnp.concatenate(pieces + [jnp.zeros(small, F32)], axis=1)

    updated, small_local = call(
        update_kernel,
        "update",
        [(block, F32), ((columns, 4 * columns), F32)],
        0,
        (ritz, basis_block, scaling, applied, right_side, correction, *received),
    )

    half = chips // 2

    def gather_half(value):
        same = [value]
        for d in range(1, half + 1):
            if d < half or chips == 1:
                pairs = [((z + d) % chips, z) for z in range(chips)]
            else:
                pairs = [(z + half, z) if z % 2 else (z, z + half) for z in range(half)]
            moves = [(2 * a + c, 2 * b + c) for a, b in pairs for c in range(2)]
            same.append(lax.ppermute(value, ROW, moves))
        other = [xor_move(v, ROW, 1) for v in same]
        return [v for pair in zip(same, other) for v in pair]

    half_blocks = gather_half(updated)
    updated_band = gather_rep(updated)
    update_small = sum_all(small_local)

    def quadratic_kernel(place_ref, rows_ref, cols_ref, tiles_ref, *refs):
        x_refs, refs = refs[: len(half_blocks)], refs[len(half_blocks) :]
        band_refs, (out_ref, xs_ref, acc_ref) = refs[:rep_count], refs[rep_count:]
        row, rep = place_ref[0], place_ref[1]
        chip, core = row // 2, row % 2
        fill_terms(x_refs, xs_ref, tiles_each, columns, 3)
        acc_ref[...] = jnp.zeros(acc_ref.shape, F32)
        takes_middle = jnp.where(chip < half, chip % 2 == 1, (chip - half) % 2 == 0)

        def index_of(j):
            col = cols_ref[j]
            owner = col // tiles_each
            distance = (owner // 2 - chip + chips) % chips
            used = (distance < half) | ((distance == half) & takes_middle)
            weight = jnp.where(distance == 0, 0.5, jnp.where(used, 1.0, 0.0)).astype(F32)
            peer = jnp.where(used, 2 * distance + lax.bitwise_xor(owner % 2, core), 0)
            return peer * tiles_each + col % tiles_each, weight

        multiply_tiles(index_of, rows_ref, tiles_ref, xs_ref, acc_ref, rep, tiles_each, columns)
        total = jnp.zeros((3 * columns, columns), F32)
        for k in range(rep_count):

            def one(t, carry, k=k):
                left = jnp.concatenate(split(acc_ref[k * tiles_each + t], 3), axis=0)
                for part in split(band_refs[k][t], 3):
                    carry = carry + dot_nt(left, part)
                return carry

            total = lax.fori_loop(0, tiles_each, one, total)
        out_ref[...] = fold(total, columns) * inverse_count

    (quadratic,) = call(
        quadratic_kernel,
        "quadratic",
        [(small, F32)],
        3,
        (place, tile_rows, tile_cols, tiles, *half_blocks, *updated_band),
        [
            pltpu.VMEM((len(half_blocks) * tiles_each, 3 * columns, tile_size), BF16),
            pltpu.VMEM((band_slots, columns, tile_size), F32),
        ],
    )
    quadratic = sum_all(quadratic)

    applied_small = basis_small[:, :columns]
    gram = basis_small[:, 2 * columns : 3 * columns]
    along = update_small[:, :columns]
    cross = full_nt(along, along)
    correction_gram = (
        update_small[:, columns : 2 * columns]
        - cross
        - cross.T
        + full_nt(full_dot(along, gram), along)
    )
    factor = jnp.linalg.cholesky(correction_gram)
    inverse = lax.linalg.triangular_solve(factor, jnp.eye(columns, dtype=F32), left_side=True, lower=True)

    def directions_kernel(inverse_ref, along_ref, updated_ref, basis_ref, out_ref):
        inverse_terms = jnp.concatenate(split(inverse_ref[...], 3), axis=0)
        along_terms = jnp.concatenate(split(along_ref[...], 3), axis=0)
        for t in range(tiles_each):
            value = updated_ref[t] - fold(dot_nn(along_terms, basis_ref[t].astype(BF16)), columns)
            total = None
            for part in split(value, 3):
                one = dot_nn(inverse_terms, part)
                total = one if total is None else total + one
            out_ref[:, t * tile_size : (t + 1) * tile_size] = fold(total, columns)

    (directions,) = call(
        directions_kernel,
        "directions",
        [((columns, shard_rows), F32)],
        0,
        (inverse, along, updated, basis_block),
    )

    def projected_kernel(quadratic_ref, inverse_ref, basis_small_ref, update_small_ref, out_ref):
        inverse_value = inverse_ref[...]
        applied_value = basis_small_ref[:, :columns]
        along_value = update_small_ref[:, :columns]
        mixed = update_small_ref[:, 2 * columns : 3 * columns]
        reduced = mixed - full_nt(along_value, applied_value)
        lower = full_dot(inverse_value, reduced)
        outer = full_nt(along_value, mixed)
        inner = full_nt(full_dot(along_value, applied_value), along_value)
        middle = quadratic_ref[...] + quadratic_ref[...].T - outer - outer.T + inner
        new = full_nt(full_dot(inverse_value, middle), inverse_value)
        out_ref[:columns, :columns] = applied_value.T
        out_ref[:columns, columns:] = lower.T
        out_ref[columns:, :columns] = lower
        out_ref[columns:, columns:] = new

    (projected,) = call(
        projected_kernel,
        "projected",
        [((2 * columns, 2 * columns), F32)],
        0,
        (quadratic, inverse, basis_small, update_small),
    )
    return (directions, projected)


def solution(mesh):
    in_specs = (
        P(None, (ROW, REP)),
        P((ROW, REP)),
        P((ROW, REP), None, None),
        P((ROW, REP)),
        P((ROW, REP)),
    )
    out_specs = (P(None, (ROW, REP)), P())
    return jax.shard_map(shards, mesh=mesh, in_specs=in_specs, out_specs=out_specs, check_vma=False)
```

time: 405 us -> 195 us (0.48)
  blocking collectives: 160 us -> 0 us
  waiting for transfers between devices: 173 us -> 75.6 us
  starting transfers between devices: 0.43 us -> 54.6 us
  Pallas kernels: 0 us -> 45 us
  matrix products: 31.4 us -> 1.3 us
  between operations: 14.4 us -> 1.03 us
  local copies, waits for them, and re-layouts: 13.9 us -> 5.83 us
    psum x4 -> x0, blocking collectives: 160 us -> none  [the longest x1 41.1 us: shards(): lax.psum(jnp.dot(correction, correction.T, precision=highest), ('row', 'r...]
    all_gather x3 -> x0, waiting for transfers between devices: 90.9 us -> none  [apply_matrix(): gathered = lax.all_gather(vectors, 'row', axis=1, tiled=True)]
    reduce_scatter x3 -> x0, waiting for transfers between devices: 81.7 us -> none  [apply_matrix(): lax.psum_scatter(partial_value, 'rep', scatter_dimension=1, tiled=True)]
    ppermute x0 -> x52, waiting for transfers between devices: none -> 75.6 us  [the longest x50 70.9 us: xor_move(): return lax.ppermute(value, axis, [(i, i ^ mask) for i in range(count)])]
    ppermute x0 -> x52, starting transfers between devices: none -> 54.6 us  [the longest x50 50.3 us: xor_move(): return lax.ppermute(value, axis, [(i, i ^ mask) for i in range(count)])]
    pallas_call x0 -> x8, Pallas kernels: none -> 45 us  [call(): pl.pallas_call(kernel, name=name, out_shape=[jax.ShapeDtypeStruct(s, d) f...]
    dot_general x18 -> x3, matrix products: 30.3 us -> 0.51 us  [the longest x2 0.3 us: full_nt(): lax.dot_general(left, right, (((1,), (1,)), ((), ())), precision=HIGHEST,...]
    reshape x3 -> x0, local copies, waits for them, and re-layouts: 5.64 us -> none  [apply_matrix(): blocks = gathered.reshape(columns, -1, tile_size)]
  transfers between devices with their start and end apart: 6 -> 52, of which waited for: 6 -> 24; matrix products, arithmetic and copies ran while one was open for 0% -> 5% of each run, Pallas kernels for 0% -> 1%
where the time goes in v1:
time: 195 us; the launch traced here: 194 us
  waiting for transfers between devices  75.6 us (39%)
  starting transfers between devices  54.6 us (28%)
  Pallas kernels  45 us (23%)
  other arithmetic  10.7 us (5%)
  local copies, waits for them, and re-layouts  5.83 us (3%)
    ppermute x50, waiting for transfers between devices, xor_move(): return lax.ppermute(value, axis, [(i, i ^ mask) for i in range(count)])  70.9 us
    ppermute x50, starting transfers between devices, xor_move(): return lax.ppermute(value, axis, [(i, i ^ mask) for i in range(count)])  50.3 us
    pallas_call x8, Pallas kernels, call(): pl.pallas_call(kernel, name=name, out_shape=[jax.ShapeDtypeStruct(s, d) f...  45 us
    unnamed x66, local copies, waits for them, and re-layouts  5.68 us
    ppermute x2, waiting for transfers between devices, gather_half(): same.append(lax.ppermute(value, ROW, moves))  4.62 us
    ppermute x2, starting transfers between devices, gather_half(): same.append(lax.ppermute(value, ROW, moves))  4.32 us
  transfers between devices with their start and end apart: 52, of which 24 were waited for; matrix products, arithmetic and copies ran while one was open for 5% of the time, Pallas kernels for 1%

profile of v1, /device:TPU:0, one launch (start us, length us, event | category | flops | bytes accessed | tf_op | source)
XLA Modules:
  0.0 194.0 jit_solution(8346771380843745548)
XLA Ops:
  0.6 1.8 prepare.1
  2.4 5.1 %collective-permute-start.5 = (f32[8,32,256]{2,1,0:T(8,128)}, f32[8,32,256]{2,1,0:T(8,128)S(1)}, u32[]{:S(2)}, u32[]{:S(2)}) collective-permute-start(f32[8,32,256]{2,1,0:T(8,128)} %get-tuple-element.19.refs_0_.basis_ref), channel_id=1, source_target_pairs={{0,24},{4,28},{8,16},{12,20},{16,8},{20,12},{24,0},{28,4},{1,25},{... | collective-permute-start | bytes 786440 | tf_op jit(solution)/shard_map/ppermute | solution.py:17
  7.5 2.4 %collective-permute-start.9 = (f32[8,40,256]{2,1,0:T(8,128)}, f32[8,40,256]{2,1,0:T(8,128)S(1)}, u32[]{:S(2)}, u32[]{:S(2)}) collective-permute-start(f32[8,40,256]{2,1,0:T(8,128)} %get-tuple-element.20.refs_8_), channel_id=1, source_target_pairs={{0,3},{1,2},{2,1},{3,0},{4,7},{5,6},{6,5},{7,4},{8,11},{9,10},{10,... | collective-permute-start | bytes 983048 | tf_op jit(solution)/shard_map/ppermute | solution.py:17
  10.7 4.2 %collective-permute-done.5.refs_6_ = f32[8,32,256]{2,1,0:T(8,128)S(1)} collective-permute-done((f32[8,32,256]{2,1,0:T(8,128)}, f32[8,32,256]{2,1,0:T(8,128)S(1)}, u32[]{:S(2)}, u32[]{:S(2)}) %collective-permute-start.5) | collective-permute-done | bytes 262176 | tf_op jit(solution)/shard_map/ppermute | solution.py:17
  16.7 13.3 %collective-permute-done.3.refs_4_ = f32[8,32,256]{2,1,0:T(8,128)S(1)} collective-permute-done((f32[8,32,256]{2,1,0:T(8,128)}, f32[8,32,256]{2,1,0:T(8,128)S(1)}, u32[]{:S(2)}, u32[]{:S(2)}) %collective-permute-start.3) | collective-permute-done | bytes 262176 | tf_op jit(solution)/shard_map/ppermute | solution.py:17
  32.7 6.3 %collective-permute-done.7.refs_9_ = f32[8,40,256]{2,1,0:T(8,128)S(1)} collective-permute-done((f32[8,40,256]{2,1,0:T(8,128)}, f32[8,40,256]{2,1,0:T(8,128)S(1)}, u32[]{:S(2)}, u32[]{:S(2)}) %collective-permute-start.7) | collective-permute-done | bytes 327712 | tf_op jit(solution)/shard_map/ppermute | solution.py:17
  40.7 13.0 %products_band.1 = (f32[8,32,256]{2,1,0:T(8,128)}, f32[8,32,256]{2,1,0:T(8,128)}, f32[8,32,256]{2,1,0:T(8,128)}, f32[8,32,256]{2,1,0:T(8,128)}, f32[32,128]{1,0:T(8,128)}) custom-call(s32[2]{0:T(128)} %pad_add_fusion.place_ref, s32[32]{0:T(128)} %rows_ref.5, s32[32]{0:T(128)} %cols_ref.5, bf16[32,256,256]{2,1,0:T(8,128)(2,1)} %tiles_ref.5, ...), custom_call_target="tpu_custom_call" | custom-call | tf_op jit(solution)/shard_map/products_band/pallas_call | solution.py:71
  55.8 2.4 %collective-permute-start.13 = (f32[32,128]{1,0:T(8,128)S(1)}, f32[32,128]{1,0:T(8,128)S(1)}, u32[]{:S(2)}, u32[]{:S(2)}) collective-permute-start(f32[32,128]{1,0:T(8,128)S(1)} %add.77), channel_id=1, source_target_pairs={{0,3},{1,2},{2,1},{3,0},{4,7},{5,6},{6,5},{7,4},{8,11},{9,10},{10,... | collective-permute-start | bytes 49160 | tf_op jit(solution)/shard_map/ppermute | solution.py:17
  62.9 2.4 %collective-permute-start.16 = (f32[32,128]{1,0:T(8,128)S(1)}, f32[32,128]{1,0:T(8,128)S(1)}, u32[]{:S(2)}, u32[]{:S(2)}) collective-permute-start(f32[32,128]{1,0:T(8,128)S(1)} %add_add_fusion.5), channel_id=1, source_target_pairs={{0,24},{4,28},{8,16},{12,20},{16,8},{20,12},{24,0},{28,4},{1,25},{... | collective-permute-start | bytes 49160 | tf_op jit(solution)/shard_map/ppermute | solution.py:17
  65.2 3.2 %collective-permute-done.16 = f32[32,128]{1,0:T(8,128)S(1)} collective-permute-done((f32[32,128]{1,0:T(8,128)S(1)}, f32[32,128]{1,0:T(8,128)S(1)}, u32[]{:S(2)}, u32[]{:S(2)}) %collective-permute-start.16) | collective-permute-done | bytes 16416 | tf_op jit(solution)/shard_map/ppermute | solution.py:17
  69.8 2.3 %collective-permute-done.14 = f32[32,128]{1,0:T(8,128)S(1)} collective-permute-done((f32[32,128]{1,0:T(8,128)S(1)}, f32[32,128]{1,0:T(8,128)S(1)}, u32[]{:S(2)}, u32[]{:S(2)}) %collective-permute-start.14) | collective-permute-done | bytes 16416 | tf_op jit(solution)/shard_map/ppermute | solution.py:17
  74.5 2.9 %correct.1 = (f32[8,32,256]{2,1,0:T(8,128)}, f32[8,32,256]{2,1,0:T(8,128)}, f32[8,32,256]{2,1,0:T(8,128)}, f32[32,1]{1,0:T(8,128)}) custom-call(f32[32,128]{1,0:T(8,128)} %add_add_fusion.4.small_ref.basis_small_ref, f32[8,32,256]{2,1,0:T(8,128)} %get-tuple-element.19.refs_0_.basis_ref, f32[8,1,256]{2,1,0:T(1,128)} %bitcast.18, ...), custom_call_target="tpu_custom_call" | custom-call | tf_op jit(solution)/shard_map/correct/pallas_call | solution.py:71
  77.4 2.3 %collective-permute-start.25 = (f32[8,32,256]{2,1,0:T(8,128)}, f32[8,32,256]{2,1,0:T(8,128)S(1)}, u32[]{:S(2)}, u32[]{:S(2)}) collective-permute-start(f32[8,32,256]{2,1,0:T(8,128)} %get-tuple-element.29.refs_0_.correction_ref), channel_id=1, source_target_pairs={{0,24},{4,28},{8,16},{12,20},{16,8},{20,12},{24,0},{28,4},{1,25},{... | collective-permute-start | bytes 786440 | tf_op jit(solution)/shard_map/ppermute | solution.py:17
  79.7 2.1 %collective-permute-start.21 = (f32[8,32,256]{2,1,0:T(8,128)}, f32[8,32,256]{2,1,0:T(8,128)S(1)}, u32[]{:S(2)}, u32[]{:S(2)}) collective-permute-start(f32[8,32,256]{2,1,0:T(8,128)} %get-tuple-element.29.refs_0_.correction_ref), channel_id=1, source_target_pairs={{0,8},{4,12},{8,0},{12,4},{16,24},{20,28},{24,16},{28,20},{1,9},{5... | collective-permute-start | bytes 786440 | tf_op jit(solution)/shard_map/ppermute | solution.py:17
  81.8 6.9 %collective-permute-done.25.refs_6_ = f32[8,32,256]{2,1,0:T(8,128)S(1)} collective-permute-done((f32[8,32,256]{2,1,0:T(8,128)}, f32[8,32,256]{2,1,0:T(8,128)S(1)}, u32[]{:S(2)}, u32[]{:S(2)}) %collective-permute-start.25) | collective-permute-done | bytes 262176 | tf_op jit(solution)/shard_map/ppermute | solution.py:17
  88.7 11.6 %collective-permute-done.23.refs_4_ = f32[8,32,256]{2,1,0:T(8,128)S(1)} collective-permute-done((f32[8,32,256]{2,1,0:T(8,128)}, f32[8,32,256]{2,1,0:T(8,128)S(1)}, u32[]{:S(2)}, u32[]{:S(2)}) %collective-permute-start.23) | collective-permute-done | bytes 262176 | tf_op jit(solution)/shard_map/ppermute | solution.py:17
  103.2 6.9 %products.1 = (f32[8,32,256]{2,1,0:T(8,128)}, f32[8,32,256]{2,1,0:T(8,128)}, f32[8,32,256]{2,1,0:T(8,128)}, f32[8,32,256]{2,1,0:T(8,128)}) custom-call(s32[2]{0:T(128)} %pad_add_fusion.place_ref, s32[32]{0:T(128)} %rows_ref.5, s32[32]{0:T(128)} %cols_ref.5, bf16[32,256,256]{2,1,0:T(8,128)(2,1)} %tiles_ref.5, ...), custom_call_target="tpu_custom_call" | custom-call | tf_op jit(solution)/shard_map/products/pallas_call | solution.py:71
  113.6 5.9 %collective-permute-done.27.refs_1_ = f32[8,32,256]{2,1,0:T(8,128)S(1)} collective-permute-done((f32[8,32,256]{2,1,0:T(8,128)}, f32[8,32,256]{2,1,0:T(8,128)S(1)}, u32[]{:S(2)}, u32[]{:S(2)}) %collective-permute-start.27) | collective-permute-done | bytes 262176 | tf_op jit(solution)/shard_map/ppermute | solution.py:17
  119.5 5.9 %collective-permute-done.28.refs_2_ = f32[8,32,256]{2,1,0:T(8,128)S(1)} collective-permute-done((f32[8,32,256]{2,1,0:T(8,128)}, f32[8,32,256]{2,1,0:T(8,128)S(1)}, u32[]{:S(2)}, u32[]{:S(2)}) %collective-permute-start.28) | collective-permute-done | bytes 262176 | tf_op jit(solution)/shard_map/ppermute | solution.py:17
  126.2 3.1 %update.1 = (f32[8,32,256]{2,1,0:T(8,128)}, f32[32,128]{1,0:T(8,128)}) custom-call(f32[32,1]{1,0:T(8,128)} %get-tuple-element.26.ritz_ref, f32[8,32,256]{2,1,0:T(8,128)} %get-tuple-element.19.refs_0_.basis_ref, f32[8,1,256]{2,1,0:T(1,128)} %bitcast.19, f32[8,32,256]{2,1,0:T(8,128)} %get-tuple-element.27.applied_ref, ...), custom_call_target="tpu_custom_call" | custom-call | tf_op jit(solution)/shard_map/update/pallas_call | solution.py:71
  137.3 1.8 collective-permute-start.36
  139.1 2.6 %collective-permute-start.34 = (f32[32,128]{1,0:T(8,128)S(1)}, f32[32,128]{1,0:T(8,128)S(1)}, u32[]{:S(2)}, u32[]{:S(2)}) collective-permute-start(f32[32,128]{1,0:T(8,128)S(1)} %add_add_fusion.3), channel_id=1, source_target_pairs={{0,8},{4,12},{8,0},{12,4},{16,24},{20,28},{24,16},{28,20},{1,9},{5... | collective-permute-start | bytes 49160 | tf_op jit(solution)/shard_map/ppermute | solution.py:17
  145.2 2.2 %collective-permute-start.40 = (f32[8,32,256]{2,1,0:T(8,128)}, f32[8,32,256]{2,1,0:T(8,128)S(1)}, u32[]{:S(2)}, u32[]{:S(2)}) collective-permute-start(f32[8,32,256]{2,1,0:T(8,128)} %get-tuple-element.35.updated_ref.refs_0_.refs_6_), channel_id=1, source_target_pairs={{0,16},{4,20},{24,8},{28,12},{1,17},{5,21},{25,9},{29,13},{2,18},{... | collective-permute-start | bytes 786440 | tf_op jit(solution)/shard_map/ppermute | solution.py:324
  147.5 2.1 %collective-permute-start.38 = (f32[8,32,256]{2,1,0:T(8,128)}, f32[8,32,256]{2,1,0:T(8,128)S(1)}, u32[]{:S(2)}, u32[]{:S(2)}) collective-permute-start(f32[8,32,256]{2,1,0:T(8,128)} %get-tuple-element.35.updated_ref.refs_0_.refs_6_), channel_id=1, source_target_pairs={{8,0},{12,4},{16,8},{20,12},{24,16},{28,20},{0,24},{4,28},{9,1},{1... | collective-permute-start | bytes 786440 | tf_op jit(solution)/shard_map/ppermute | solution.py:324
  151.8 1.8 collective-permute-done.40.refs_4_
  153.6 2.8 %collective-permute-done.38.refs_2_ = f32[8,32,256]{2,1,0:T(8,128)S(1)} collective-permute-done((f32[8,32,256]{2,1,0:T(8,128)}, f32[8,32,256]{2,1,0:T(8,128)S(1)}, u32[]{:S(2)}, u32[]{:S(2)}) %collective-permute-start.38) | collective-permute-done | bytes 262176 | tf_op jit(solution)/shard_map/ppermute | solution.py:324
  156.4 2.9 %cholesky.17 = f32[32,32]{1,0:T(8,128)S(1)} custom-call(f32[32,32]{1,0:T(8,128)S(1)} %fusion.7), custom_call_target="Cholesky" | custom-call | tf_op jit(solution)/shard_map/jit(cholesky)/cholesky | solution.py:386
  161.1 12.0 %quadratic.1 = f32[32,32]{1,0:T(8,128)} custom-call(s32[2]{0:T(128)} %pad_add_fusion.place_ref, s32[32]{0:T(128)} %rows_ref.5, s32[32]{0:T(128)} %cols_ref.5, bf16[32,256,256]{2,1,0:T(8,128)(2,1)} %tiles_ref.5, f32[8,32,256]{2,1,0:T(8,128)} %get-tuple-element.35.updated_ref.refs_0_.refs_6_, f32[8,32,256]{2,1,0:T(8,128)} %copy-done.19, ...), custom_call_target="tpu_custom_call" | custom-call | tf_op jit(solution)/shard_map/quadratic/pallas_call | solution.py:71
  179.6 2.4 %custom-call.6 = f32[1,32,32]{1,2,0:T(8,128)S(1)} custom-call(f32[1,32,32]{2,1,0:T(8,128)S(1)} %fusion), custom_call_target="InvertDiagBlocksLowerTriangular" | custom-call | tf_op jit(solution)/shard_map/triangular_solve | solution.py:387
  182.1 4.2 %collective-permute-start.51 = (f32[32,32]{1,0:T(8,128)S(1)}, f32[32,32]{1,0:T(8,128)S(1)}, u32[]{:S(2)}, u32[]{:S(2)}) collective-permute-start(f32[32,32]{1,0:T(8,128)S(1)} %add_add_fusion.1), channel_id=1, source_target_pairs={{0,24},{4,28},{8,16},{12,20},{16,8},{20,12},{24,0},{28,4},{1,25},{... | collective-permute-start | bytes 12296 | tf_op jit(solution)/shard_map/ppermute | solution.py:17
  187.8 2.9 %directions.1 = f32[32,2048]{1,0:T(8,128)} custom-call(f32[32,32]{1,0:T(8,128)} %fusion.5.inverse_ref, f32[32,32]{1,0:T(8,128)} %bitcast.16, f32[8,32,256]{2,1,0:T(8,128)} %get-tuple-element.35.updated_ref.refs_0_.refs_6_, f32[8,32,256]{2,1,0:T(8,128)} %get-tuple-element.19.refs_0_.basis_ref), custom_call_target="tpu_custom_call" | custom-call | tf_op jit(solution)/shard_map/directions/pallas_call | solution.py:71
  191.6 2.4 %projected.1 = f32[64,64]{1,0:T(8,128)} custom-call(f32[32,32]{1,0:T(8,128)} %add_add_fusion.quadratic_ref, f32[32,32]{1,0:T(8,128)} %fusion.5.inverse_ref, f32[32,128]{1,0:T(8,128)} %add_add_fusion.4.small_ref.basis_small_ref, f32[32,128]{1,0:T(8,128)} %copy-done), custom_call_target="tpu_custom_call" | custom-call | tf_op jit(solution)/shard_map/projected/pallas_call | solution.py:71
  (168 shorter events, 48.6 us)
Async XLA Ops:
  2.4 12.5 %collective-permute-start.5 = (f32[8,32,256]{2,1,0:T(8,128)}, f32[8,32,256]{2,1,0:T(8,128)S(1)}, u32[]{:S(2)}, u32[]{:S(2)}) collective-permute-start(f32[8,32,256]{2,1,0:T(8,128)} %get-tuple-element.19.refs_0_.basis_ref), channel_id=1, source_target_pairs={{0,24},{4,28},{8,16},{12,20},{16,8},{20,12},{24,0},{28,4},{1,25},{... | collective-permute-start | bytes 786440 | tf_op jit(solution)/shard_map/ppermute | solution.py:17
  7.5 22.5 %collective-permute-start.3 = (f32[8,32,256]{2,1,0:T(8,128)}, f32[8,32,256]{2,1,0:T(8,128)S(1)}, u32[]{:S(2)}, u32[]{:S(2)}) collective-permute-start(f32[8,32,256]{2,1,0:T(8,128)} %get-tuple-element.19.refs_0_.basis_ref), channel_id=1, source_target_pairs={{0,16},{4,20},{8,24},{12,28},{16,0},{20,4},{24,8},{28,12},{1,17},{... | collective-permute-start | bytes 786440 | tf_op jit(solution)/shard_map/ppermute | solution.py:17
  7.5 24.5 %collective-permute-start.9 = (f32[8,40,256]{2,1,0:T(8,128)}, f32[8,40,256]{2,1,0:T(8,128)S(1)}, u32[]{:S(2)}, u32[]{:S(2)}) collective-permute-start(f32[8,40,256]{2,1,0:T(8,128)} %get-tuple-element.20.refs_8_), channel_id=1, source_target_pairs={{0,3},{1,2},{2,1},{3,0},{4,7},{5,6},{6,5},{7,4},{8,11},{9,10},{10,... | collective-permute-start | bytes 983048 | tf_op jit(solution)/shard_map/ppermute | solution.py:17
  9.9 21.6 %collective-permute-start.1 = (f32[8,32,256]{2,1,0:T(8,128)}, f32[8,32,256]{2,1,0:T(8,128)S(1)}, u32[]{:S(2)}, u32[]{:S(2)}) collective-permute-start(f32[8,32,256]{2,1,0:T(8,128)} %get-tuple-element.19.refs_0_.basis_ref), channel_id=1, source_target_pairs={{0,8},{4,12},{8,0},{12,4},{16,24},{20,28},{24,16},{28,20},{1,9},{5... | collective-permute-start | bytes 786440 | tf_op jit(solution)/shard_map/ppermute | solution.py:17
  10.7 20.8 %collective-permute-start = (f32[8,32,256]{2,1,0:T(8,128)}, f32[8,32,256]{2,1,0:T(8,128)S(1)}, u32[]{:S(2)}, u32[]{:S(2)}) collective-permute-start(f32[8,32,256]{2,1,0:T(8,128)} %get-tuple-element.19.refs_0_.basis_ref), channel_id=1, source_target_pairs={{0,4},{4,0},{8,12},{12,8},{16,20},{20,16},{24,28},{28,24},{1,5},{5... | collective-permute-start | bytes 786440 | tf_op jit(solution)/shard_map/ppermute | solution.py:17
  15.0 17.7 %collective-permute-start.8 = (f32[8,40,256]{2,1,0:T(8,128)}, f32[8,40,256]{2,1,0:T(8,128)S(1)}, u32[]{:S(2)}, u32[]{:S(2)}) collective-permute-start(f32[8,40,256]{2,1,0:T(8,128)} %get-tuple-element.20.refs_8_), channel_id=1, source_target_pairs={{0,2},{1,3},{2,0},{3,1},{4,6},{5,7},{6,4},{7,5},{8,10},{9,11},{10,... | collective-permute-start | bytes 983048 | tf_op jit(solution)/shard_map/ppermute | solution.py:17
  30.0 9.0 %collective-permute-start.7 = (f32[8,40,256]{2,1,0:T(8,128)}, f32[8,40,256]{2,1,0:T(8,128)S(1)}, u32[]{:S(2)}, u32[]{:S(2)}) collective-permute-start(f32[8,40,256]{2,1,0:T(8,128)} %get-tuple-element.20.refs_8_), channel_id=1, source_target_pairs={{0,1},{1,0},{2,3},{3,2},{4,5},{5,4},{6,7},{7,6},{8,9},{9,8},{10,11... | collective-permute-start | bytes 983048 | tf_op jit(solution)/shard_map/ppermute | solution.py:17
  31.5 7.5 %collective-permute-start.6 = (f32[8,32,256]{2,1,0:T(8,128)S(1)}, f32[8,32,256]{2,1,0:T(8,128)S(1)}, u32[]{:S(2)}, u32[]{:S(2)}) collective-permute-start(f32[8,32,256]{2,1,0:T(8,128)S(1)} %collective-permute-done.5.refs_6_), channel_id=1, source_target_pairs={{0,4},{4,0},{8,12},{12,8},{16,20},{20,16},{24,28},{28,24},{1,5},{5... | collective-permute-start | bytes 786440 | tf_op jit(solution)/shard_map/ppermute | solution.py:17
  31.5 7.5 %collective-permute-start.4 = (f32[8,32,256]{2,1,0:T(8,128)S(1)}, f32[8,32,256]{2,1,0:T(8,128)S(1)}, u32[]{:S(2)}, u32[]{:S(2)}) collective-permute-start(f32[8,32,256]{2,1,0:T(8,128)S(1)} %collective-permute-done.3.refs_4_), channel_id=1, source_target_pairs={{0,4},{4,0},{8,12},{12,8},{16,20},{20,16},{24,28},{28,24},{1,5},{5... | collective-permute-start | bytes 786440 | tf_op jit(solution)/shard_map/ppermute | solution.py:17
  32.0 7.0 %collective-permute-start.2 = (f32[8,32,256]{2,1,0:T(8,128)S(1)}, f32[8,32,256]{2,1,0:T(8,128)S(1)}, u32[]{:S(2)}, u32[]{:S(2)}) collective-permute-start(f32[8,32,256]{2,1,0:T(8,128)S(1)} %collective-permute-done.1.refs_2_), channel_id=1, source_target_pairs={{0,4},{4,0},{8,12},{12,8},{16,20},{20,16},{24,28},{28,24},{1,5},{5... | collective-permute-start | bytes 786440 | tf_op jit(solution)/shard_map/ppermute | solution.py:17
  55.8 6.5 %collective-permute-start.13 = (f32[32,128]{1,0:T(8,128)S(1)}, f32[32,128]{1,0:T(8,128)S(1)}, u32[]{:S(2)}, u32[]{:S(2)}) collective-permute-start(f32[32,128]{1,0:T(8,128)S(1)} %add.77), channel_id=1, source_target_pairs={{0,3},{1,2},{2,1},{3,0},{4,7},{5,6},{6,5},{7,4},{8,11},{9,10},{10,... | collective-permute-start | bytes 49160 | tf_op jit(solution)/shard_map/ppermute | solution.py:17
  59.2 13.6 %collective-permute-start.17 = (f32[8,32,256]{2,1,0:T(8,128)}, f32[8,32,256]{2,1,0:T(8,128)S(1)}, u32[]{:S(2)}, u32[]{:S(2)}) collective-permute-start(f32[8,32,256]{2,1,0:T(8,128)} %get-tuple-element.23), channel_id=1, source_target_pairs={{0,1},{1,0},{2,3},{3,2},{4,5},{5,4},{6,7},{7,6},{8,9},{9,8},{10,11... | collective-permute-start | bytes 786440 | tf_op jit(solution)/shard_map/ppermute | solution.py:17
  60.8 12.2 %collective-permute-start.18 = (f32[8,32,256]{2,1,0:T(8,128)}, f32[8,32,256]{2,1,0:T(8,128)S(1)}, u32[]{:S(2)}, u32[]{:S(2)}) collective-permute-start(f32[8,32,256]{2,1,0:T(8,128)} %get-tuple-element.24), channel_id=1, source_target_pairs={{0,2},{1,3},{2,0},{3,1},{4,6},{5,7},{6,4},{7,5},{8,10},{9,11},{10,... | collective-permute-start | bytes 786440 | tf_op jit(solution)/shard_map/ppermute | solution.py:17
  62.3 11.6 %collective-permute-start.19 = (f32[8,32,256]{2,1,0:T(8,128)}, f32[8,32,256]{2,1,0:T(8,128)S(1)}, u32[]{:S(2)}, u32[]{:S(2)}) collective-permute-start(f32[8,32,256]{2,1,0:T(8,128)} %get-tuple-element.25), channel_id=1, source_target_pairs={{0,3},{1,2},{2,1},{3,0},{4,7},{5,6},{6,5},{7,4},{8,11},{9,10},{10,... | collective-permute-start | bytes 786440 | tf_op jit(solution)/shard_map/ppermute | solution.py:17
  77.4 11.3 %collective-permute-start.25 = (f32[8,32,256]{2,1,0:T(8,128)}, f32[8,32,256]{2,1,0:T(8,128)S(1)}, u32[]{:S(2)}, u32[]{:S(2)}) collective-permute-start(f32[8,32,256]{2,1,0:T(8,128)} %get-tuple-element.29.refs_0_.correction_ref), channel_id=1, source_target_pairs={{0,24},{4,28},{8,16},{12,20},{16,8},{20,12},{24,0},{28,4},{1,25},{... | collective-permute-start | bytes 786440 | tf_op jit(solution)/shard_map/ppermute | solution.py:17
  79.7 20.6 %collective-permute-start.23 = (f32[8,32,256]{2,1,0:T(8,128)}, f32[8,32,256]{2,1,0:T(8,128)S(1)}, u32[]{:S(2)}, u32[]{:S(2)}) collective-permute-start(f32[8,32,256]{2,1,0:T(8,128)} %get-tuple-element.29.refs_0_.correction_ref), channel_id=1, source_target_pairs={{0,16},{4,20},{8,24},{12,28},{16,0},{20,4},{24,8},{28,12},{1,17},{... | collective-permute-start | bytes 786440 | tf_op jit(solution)/shard_map/ppermute | solution.py:17
  79.7 20.6 %collective-permute-start.21 = (f32[8,32,256]{2,1,0:T(8,128)}, f32[8,32,256]{2,1,0:T(8,128)S(1)}, u32[]{:S(2)}, u32[]{:S(2)}) collective-permute-start(f32[8,32,256]{2,1,0:T(8,128)} %get-tuple-element.29.refs_0_.correction_ref), channel_id=1, source_target_pairs={{0,8},{4,12},{8,0},{12,4},{16,24},{20,28},{24,16},{28,20},{1,9},{5... | collective-permute-start | bytes 786440 | tf_op jit(solution)/shard_map/ppermute | solution.py:17
  81.8 19.0 %collective-permute-start.20 = (f32[8,32,256]{2,1,0:T(8,128)}, f32[8,32,256]{2,1,0:T(8,128)S(1)}, u32[]{:S(2)}, u32[]{:S(2)}) collective-permute-start(f32[8,32,256]{2,1,0:T(8,128)} %get-tuple-element.29.refs_0_.correction_ref), channel_id=1, source_target_pairs={{0,4},{4,0},{8,12},{12,8},{16,20},{20,16},{24,28},{28,24},{1,5},{5... | collective-permute-start | bytes 786440 | tf_op jit(solution)/shard_map/ppermute | solution.py:17
  88.7 12.1 %collective-permute-start.26 = (f32[8,32,256]{2,1,0:T(8,128)S(1)}, f32[8,32,256]{2,1,0:T(8,128)S(1)}, u32[]{:S(2)}, u32[]{:S(2)}) collective-permute-start(f32[8,32,256]{2,1,0:T(8,128)S(1)} %collective-permute-done.25.refs_6_), channel_id=1, source_target_pairs={{0,4},{4,0},{8,12},{12,8},{16,20},{20,16},{24,28},{28,24},{1,5},{5... | collective-permute-start | bytes 786440 | tf_op jit(solution)/shard_map/ppermute | solution.py:17
  110.1 9.4 %collective-permute-start.27 = (f32[8,32,256]{2,1,0:T(8,128)}, f32[8,32,256]{2,1,0:T(8,128)S(1)}, u32[]{:S(2)}, u32[]{:S(2)}) collective-permute-start(f32[8,32,256]{2,1,0:T(8,128)} %get-tuple-element.31), channel_id=1, source_target_pairs={{0,1},{1,0},{2,3},{3,2},{4,5},{5,4},{6,7},{7,6},{8,9},{9,8},{10,11... | collective-permute-start | bytes 786440 | tf_op jit(solution)/shard_map/ppermute | solution.py:17
  111.5 13.9 %collective-permute-start.28 = (f32[8,32,256]{2,1,0:T(8,128)}, f32[8,32,256]{2,1,0:T(8,128)S(1)}, u32[]{:S(2)}, u32[]{:S(2)}) collective-permute-start(f32[8,32,256]{2,1,0:T(8,128)} %get-tuple-element.32), channel_id=1, source_target_pairs={{0,2},{1,3},{2,0},{3,1},{4,6},{5,7},{6,4},{7,5},{8,10},{9,11},{10,... | collective-permute-start | bytes 786440 | tf_op jit(solution)/shard_map/ppermute | solution.py:17
  112.0 13.4 %collective-permute-start.29 = (f32[8,32,256]{2,1,0:T(8,128)}, f32[8,32,256]{2,1,0:T(8,128)S(1)}, u32[]{:S(2)}, u32[]{:S(2)}) collective-permute-start(f32[8,32,256]{2,1,0:T(8,128)} %get-tuple-element.33), channel_id=1, source_target_pairs={{0,3},{1,2},{2,1},{3,0},{4,7},{5,6},{6,5},{7,4},{8,11},{9,10},{10,... | collective-permute-start | bytes 786440 | tf_op jit(solution)/shard_map/ppermute | solution.py:17
  137.3 7.3 %collective-permute-start.36 = (f32[32,128]{1,0:T(8,128)S(1)}, f32[32,128]{1,0:T(8,128)S(1)}, u32[]{:S(2)}, u32[]{:S(2)}) collective-permute-start(f32[32,128]{1,0:T(8,128)S(1)} %add_add_fusion.3), channel_id=1, source_target_pairs={{0,24},{4,28},{8,16},{12,20},{16,8},{20,12},{24,0},{28,4},{1,25},{... | collective-permute-start | bytes 49160 | tf_op jit(solution)/shard_map/ppermute | solution.py:17
  139.1 8.3 %collective-permute-start.34 = (f32[32,128]{1,0:T(8,128)S(1)}, f32[32,128]{1,0:T(8,128)S(1)}, u32[]{:S(2)}, u32[]{:S(2)}) collective-permute-start(f32[32,128]{1,0:T(8,128)S(1)} %add_add_fusion.3), channel_id=1, source_target_pairs={{0,8},{4,12},{8,0},{12,4},{16,24},{20,28},{24,16},{28,20},{1,9},{5... | collective-permute-start | bytes 49160 | tf_op jit(solution)/shard_map/ppermute | solution.py:17
  141.7 10.1 %collective-permute-start.44 = (f32[8,32,256]{2,1,0:T(8,128)}, f32[8,32,256]{2,1,0:T(8,128)S(1)}, u32[]{:S(2)}, u32[]{:S(2)}) collective-permute-start(f32[8,32,256]{2,1,0:T(8,128)} %get-tuple-element.35.updated_ref.refs_0_.refs_6_), channel_id=1, source_target_pairs={{0,3},{1,2},{2,1},{3,0},{4,7},{5,6},{6,5},{7,4},{8,11},{9,10},{10,... | collective-permute-start | bytes 786440 | tf_op jit(solution)/shard_map/ppermute | solution.py:17
  143.1 16.3 %collective-permute-start.43 = (f32[8,32,256]{2,1,0:T(8,128)}, f32[8,32,256]{2,1,0:T(8,128)S(1)}, u32[]{:S(2)}, u32[]{:S(2)}) collective-permute-start(f32[8,32,256]{2,1,0:T(8,128)} %get-tuple-element.35.updated_ref.refs_0_.refs_6_), channel_id=1, source_target_pairs={{0,2},{1,3},{2,0},{3,1},{4,6},{5,7},{6,4},{7,5},{8,10},{9,11},{10,... | collective-permute-start | bytes 786440 | tf_op jit(solution)/shard_map/ppermute | solution.py:17
  144.6 14.8 %collective-permute-start.42 = (f32[8,32,256]{2,1,0:T(8,128)}, f32[8,32,256]{2,1,0:T(8,128)S(1)}, u32[]{:S(2)}, u32[]{:S(2)}) collective-permute-start(f32[8,32,256]{2,1,0:T(8,128)} %get-tuple-element.35.updated_ref.refs_0_.refs_6_), channel_id=1, source_target_pairs={{0,1},{1,0},{2,3},{3,2},{4,5},{5,4},{6,7},{7,6},{8,9},{9,8},{10,11... | collective-permute-start | bytes 786440 | tf_op jit(solution)/shard_map/ppermute | solution.py:17
  145.2 8.4 %collective-permute-start.40 = (f32[8,32,256]{2,1,0:T(8,128)}, f32[8,32,256]{2,1,0:T(8,128)S(1)}, u32[]{:S(2)}, u32[]{:S(2)}) collective-permute-start(f32[8,32,256]{2,1,0:T(8,128)} %get-tuple-element.35.updated_ref.refs_0_.refs_6_), channel_id=1, source_target_pairs={{0,16},{4,20},{24,8},{28,12},{1,17},{5,21},{25,9},{29,13},{2,18},{... | collective-permute-start | bytes 786440 | tf_op jit(solution)/shard_map/ppermute | solution.py:324
  147.5 9.0 %collective-permute-start.38 = (f32[8,32,256]{2,1,0:T(8,128)}, f32[8,32,256]{2,1,0:T(8,128)S(1)}, u32[]{:S(2)}, u32[]{:S(2)}) collective-permute-start(f32[8,32,256]{2,1,0:T(8,128)} %get-tuple-element.35.updated_ref.refs_0_.refs_6_), channel_id=1, source_target_pairs={{8,0},{12,4},{16,8},{20,12},{24,16},{28,20},{0,24},{4,28},{9,1},{1... | collective-permute-start | bytes 786440 | tf_op jit(solution)/shard_map/ppermute | solution.py:324
  151.8 7.6 %collective-permute-start.37 = (f32[8,32,256]{2,1,0:T(8,128)}, f32[8,32,256]{2,1,0:T(8,128)S(1)}, u32[]{:S(2)}, u32[]{:S(2)}) collective-permute-start(f32[8,32,256]{2,1,0:T(8,128)} %get-tuple-element.35.updated_ref.refs_0_.refs_6_), channel_id=1, source_target_pairs={{0,4},{4,0},{8,12},{12,8},{16,20},{20,16},{24,28},{28,24},{1,5},{5... | collective-permute-start | bytes 786440 | tf_op jit(solution)/shard_map/ppermute | solution.py:17
  175.4 6.6 %collective-permute-start.48 = (f32[32,32]{1,0:T(8,128)S(1)}, f32[32,32]{1,0:T(8,128)S(1)}, u32[]{:S(2)}, u32[]{:S(2)}) collective-permute-start(f32[32,32]{1,0:T(8,128)S(1)} %add.93), channel_id=1, source_target_pairs={{0,3},{1,2},{2,1},{3,0},{4,7},{5,6},{6,5},{7,4},{8,11},{9,10},{10,... | collective-permute-start | bytes 12296 | tf_op jit(solution)/shard_map/ppermute | solution.py:17
  182.1 8.6 %collective-permute-start.51 = (f32[32,32]{1,0:T(8,128)S(1)}, f32[32,32]{1,0:T(8,128)S(1)}, u32[]{:S(2)}, u32[]{:S(2)}) collective-permute-start(f32[32,32]{1,0:T(8,128)S(1)} %add_add_fusion.1), channel_id=1, source_target_pairs={{0,24},{4,28},{8,16},{12,20},{16,8},{20,12},{24,0},{28,4},{1,25},{... | collective-permute-start | bytes 12296 | tf_op jit(solution)/shard_map/ppermute | solution.py:17
  (53 other events, 303.6 us)
